TPU v7x, 32 devices: a whole 2x2x4 slice. The times are simulated.
32 devices in a mesh: ctx: 4 (over z), exp: 8 (over y, x, core).
Axes of the slice: x: 2, y: 2, z: 4, core: 2. Of those that a mesh axis runs over, the one named last changes fastest.
Arguments:
- seq_inputs: bfloat16 [2048, 2048], P('ctx', 'exp'), may hold values from -6 to 6
- step_size: float32 [32, 2048], P('exp', 'ctx'), may hold values from 0.0007 to 0.14
- write_map: bfloat16 [16, 2048], P(None, 'ctx'), may hold values from -2 to 2
- read_map: bfloat16 [16, 2048], P(None, 'ctx'), may hold values from -2 to 2
- decay_log: float32 [32], P('exp'), may hold values from -9.3 to 1.4
- skip_gain: float32 [32], P('exp'), may hold values from 0.5 to 1.5
- moe_tokens: bfloat16 [1024, 4096], P('exp'), may hold values from -6 to 6
- expert_ids: int32 [1024, 2], P('exp'), may hold values from 0 to 3, all different within a row; in each aligned block of 128 rows (0 to 127, 128 to 255, ...) at most 128 rows name the same one
- route_weights: float32 [1024, 2], P('exp'), may hold values from 0.1 to 1
- gate_proj: bfloat16 [8, 4096, 3584], P('exp', None, 'ctx'), may hold values from -0.09375 to 0.09375
- up_proj: bfloat16 [8, 4096, 3584], P('exp', None, 'ctx'), may hold values from -0.09375 to 0.09375
- down_proj: bfloat16 [8, 3584, 4096], P('exp', None, 'ctx'), may hold values from -0.0625 to 0.0625
Outputs:
- mixer_output: bfloat16 [2048, 2048], P('ctx', 'exp')
- expert_output: bfloat16 [1024, 4096], P('exp', 'ctx')
Inputs may be any that keep to these rules, and one draw needn't show every extreme that they name: `expert_ids`: each row names two different experts. In the 128 rows of one index of exp (aligned blocks), no expert is named more than 128 times, and in some blocks an expert is named exactly 128 times.
All inputs are finite; a program needn't handle non-finite values.
Results may differ from a plain program's by a relative error of at most 0.002.
The roundings to bfloat16 on the way count: a program that leaves them out, or rounds other values in their place, can miss the bound.
Values may be sent and summed in bfloat16 or wider, within the bound.
A program may use at most 64 MiB of HBM per device.

v0:
```python
import jax
import jax.numpy as jnp
from jax import lax
from jax.sharding import PartitionSpec as P

BLOCK = 256


HIGHEST = lax.Precision.HIGHEST


def carried_in(part, axis, combine, identity):
    place = lax.axis_index(axis)
    gathered = jax.tree.map(lambda a: lax.all_gather(a, axis), part)
    state = jax.tree.map(lambda a, e: jnp.zeros_like(a) + jnp.asarray(e, a.dtype), part, identity)

    def one(lap, state):
        return combine(
            state, jax.tree.map(lambda a: lax.dynamic_index_in_dim(a, lap, 0, False), gathered)
        )

    return lax.fori_loop(0, place, one, state)


def combine_states(former, latter):
    return (former[0] + latter[0], jnp.exp(latter[0])[:, None, None] * former[1] + latter[1])


def block_chain(running, pieces):
    decay, increment = pieces
    return (decay[:, None, None] * running + increment, running)


def mixer_prepare(seq_inputs, step_size, write_map, read_map, decay_log):
    length = seq_inputs.shape[0]
    head_count = step_size.shape[0]
    state_count = write_map.shape[0]
    head_width = seq_inputs.shape[1] // head_count
    block_count = length // BLOCK
    decay_rate = -jnp.exp(decay_log)
    log_decay = (step_size * decay_rate[:, None]).reshape(head_count, block_count, BLOCK)
    cumulative = jnp.cumsum(log_decay, axis=2)
    block_ends = cumulative[:, :, BLOCK - 1]
    step_blocks = step_size.reshape(head_count, block_count, BLOCK)
    write_blocks = write_map.reshape(state_count, block_count, BLOCK)
    read_blocks = read_map.reshape(state_count, block_count, BLOCK)
    value_blocks = seq_inputs.reshape(block_count, BLOCK, head_count, head_width)
    scores = jnp.einsum(
        "nkt,nks->kts", read_blocks, write_blocks, preferred_element_type=jnp.float32
    )
    row_index = lax.broadcasted_iota(jnp.int32, (BLOCK, BLOCK), 0)
    column_index = lax.broadcasted_iota(jnp.int32, (BLOCK, BLOCK), 1)
    lower = column_index <= row_index
    difference = cumulative[:, :, :, None] - cumulative[:, :, None, :]
    decay = jnp.where(lower[None, None], jnp.exp(jnp.minimum(difference, 0.0)), 0.0)
    mixing = (scores[None] * decay * step_blocks[:, :, None, :]).astype(jnp.bfloat16)
    local_mix = jnp.einsum(
        "hkts,kshp->kthp", mixing, value_blocks, preferred_element_type=jnp.float32
    )
    weights = jnp.exp(block_ends[:, :, None] - cumulative) * step_blocks
    key_decayed = (write_blocks[None] * weights[:, None]).astype(jnp.bfloat16)
    increments = jnp.einsum(
        "hnks,kshp->khnp", key_decayed, value_blocks, preferred_element_type=jnp.float32
    )
    zero_state = jnp.zeros((head_count, state_count, head_width), jnp.float32)
    final, entering = lax.scan(block_chain, zero_state, (jnp.exp(block_ends).T, increments))
    return (local_mix, cumulative, block_ends, entering, final)


def mixer_finish(
    local_mix, cumulative, block_ends, entering, state_before, read_map, seq_inputs, skip_gain
):
    head_count = block_ends.shape[0]
    block_count = block_ends.shape[1]
    state_count = read_map.shape[0]
    head_width = entering.shape[3]
    before = jnp.cumsum(block_ends, axis=1) - block_ends
    states = jnp.exp(before).T[:, :, None, None] * state_before[None] + entering
    read_blocks = read_map.reshape(state_count, block_count, BLOCK).astype(jnp.float32)
    carried = jnp.einsum("nkt,khnp->kthp", read_blocks, states, precision=HIGHEST)
    carried = carried * jnp.exp(cumulative).transpose(1, 2, 0)[:, :, :, None]
    value_blocks = seq_inputs.reshape(block_count, BLOCK, head_count, head_width).astype(
        jnp.float32
    )
    output = local_mix + carried + skip_gain[None, None, :, None] * value_blocks
    return output.reshape(seq_inputs.shape).astype(jnp.bfloat16)


def expert_block(moe_tokens, expert_ids, route_weights, gate_proj, up_proj, down_proj):
    group_size = moe_tokens.shape[0]
    model_width = moe_tokens.shape[1]
    expert_count = lax.axis_size("exp") // 2
    capacity = min(group_size, 4 * group_size // expert_count)
    slot_count = expert_count * capacity
    assigned = expert_ids.reshape(group_size * 2)
    onehot = (
        assigned[:, None] == lax.broadcasted_iota(jnp.int32, (group_size * 2, expert_count), 1)
    ).astype(jnp.int32)
    earlier_count = jnp.cumsum(onehot, axis=0) - onehot
    position = jnp.sum((earlier_count + assigned[:, None] * capacity) * onehot, axis=1)
    matches = (
        position[:, None] == lax.broadcasted_iota(jnp.int32, (group_size * 2, slot_count), 1)
    ).astype(jnp.float32)
    dispatch = jnp.sum(matches.reshape(group_size, 2, slot_count), axis=1).astype(jnp.bfloat16)
    combine = jnp.sum(
        (matches * route_weights.reshape(group_size * 2)[:, None]).reshape(
            group_size, 2, slot_count
        ),
        axis=1,
    )
    gate_weight = gate_proj[0]
    up_weight = up_proj[0]
    down_weight = down_proj[0]
    packed = jnp.einsum(
        "is,id->sd", dispatch, moe_tokens, preferred_element_type=jnp.float32
    ).astype(jnp.bfloat16)
    doubled = jnp.broadcast_to(
        packed.reshape(expert_count, 1, capacity, model_width),
        (expert_count, 2, capacity, model_width),
    )
    arrived = lax.all_to_all(
        doubled.reshape(2 * slot_count, model_width), "exp", split_axis=0, concat_axis=0, tiled=True
    )
    gate_sums = jnp.dot(arrived, gate_weight, preferred_element_type=jnp.float32)
    up_sums = jnp.dot(arrived, up_weight, preferred_element_type=jnp.float32)
    hidden = (jax.nn.silu(gate_sums) * up_sums).astype(jnp.bfloat16)
    partial_out = jnp.dot(
        lax.all_gather(hidden, "ctx", axis=1, tiled=True),
        down_weight,
        preferred_element_type=jnp.float32,
    )
    returned = lax.all_to_all(partial_out, "exp", split_axis=0, concat_axis=0, tiled=True)
    summed = jnp.sum(returned.reshape(expert_count, 2, capacity, -1), axis=1).reshape(
        slot_count, -1
    )
    result = jnp.dot(combine, summed, precision=HIGHEST, preferred_element_type=jnp.float32)
    return result.astype(jnp.bfloat16)


def on_device(
    seq_inputs,
    step_size,
    write_map,
    read_map,
    decay_log,
    skip_gain,
    moe_tokens,
    expert_ids,
    route_weights,
    gate_proj,
    up_proj,
    down_proj,
):
    local_mix, cumulative, block_ends, entering, final = mixer_prepare(
        seq_inputs, step_size, write_map, read_map, decay_log
    )
    total_log = jnp.sum(block_ends, axis=1)
    log_before, state_before = carried_in(
        (total_log, final),
        "ctx",
        combine_states,
        (jnp.zeros_like(total_log), jnp.zeros_like(final)),
    )
    expert_output = expert_block(
        moe_tokens, expert_ids, route_weights, gate_proj, up_proj, down_proj
    )
    mixer_output = mixer_finish(
        local_mix, cumulative, block_ends, entering, state_before, read_map, seq_inputs, skip_gain
    )
    return (mixer_output, expert_output)


def solution(mesh):
    return jax.shard_map(
        on_device,
        mesh=mesh,
        in_specs=(
            P("ctx", "exp"),
            P("exp", "ctx"),
            P(None, "ctx"),
            P(None, "ctx"),
            P("exp"),
            P("exp"),
            P("exp", None),
            P("exp", None),
            P("exp", None),
            P("exp", None, "ctx"),
            P("exp", None, "ctx"),
            P("exp", None, "ctx"),
        ),
        out_specs=(P("ctx", "exp"), P("exp", "ctx")),
        check_vma=False,
    )
```

profile of v0, /device:TPU:0, one launch (start us, length us, event | category | flops | bytes accessed | tf_op | source)
XLA Modules:
  0.0 352.8 jit_solution(9467480239295437429)
XLA Ops:
  7.2 0.9 copy.92
  8.4 1.2 reduce-window.16
  10.2 0.9 convert_reduce_fusion
  11.2 1.3 convolution_convert_fusion
  12.4 4.3 %broadcast_in_dim.26 = bf16[4,2,128,4096]{3,2,1,0:T(8,128)(2,1)} broadcast(bf16[4,128,4096]{2,1,0:T(8,128)(2,1)S(1)} %bitcast.106), dimensions={0,2,3} | broadcast | bytes 12582912 | tf_op jit(solution)/shard_map/broadcast_in_dim | solution.py:117
  16.7 99.4 %all_to_all.18 = bf16[8,128,4096]{2,1,0:T(8,128)(2,1)S(1)} all-to-all(bf16[8,128,4096]{2,1,0:T(8,128)(2,1)} %bitcast.105), channel_id=1, replica_groups=mesh['ctx'=4,'exp'=8] {'exp'}, dimensions={0} | all-to-all | bytes 16777216 | tf_op jit(solution)/shard_map/all_to_all | solution.py:121
  116.2 15.1 %fusion.3 = f32[1024,896]{1,0:T(8,128)S(1)} fusion(bf16[1024,4096]{1,0:T(8,128)(2,1)S(1)} %bitcast.108, bf16[1,4096,896]{2,1,0:T(8,128)(2,1)} %param.26), kind=kOutput, calls=%fused_computation.8 | convolution fusion | flops 7516192768 | bytes 19398656 | tf_op jit(solution)/shard_map/dot_general | solution.py:125
  131.3 10.4 %multiply_convert_fusion = bf16[1024,896]{1,0:T(8,128)(2,1)} fusion(f32[1024,896]{1,0:T(8,128)S(1)} %fusion.3, bf16[1024,4096]{1,0:T(8,128)(2,1)S(1)} %bitcast.109, bf16[1,4096,896]{2,1,0:T(8,128)(2,1)S(1)} %bitcast.120), kind=kOutput, calls=%fused_computation.14 | convolution fusion | flops 7521697792 | bytes 21233664 | tf_op jit(solution)/shard_map/dot_general | solution.py:124
  141.8 2.4 reduce-window.14
  145.5 0.3 copy.82
  146.0 127.8 %all-gather.4.cloned.1.call-done = bf16[1024,3584]{1,0:T(8,128)(2,1)} async-done(((bf16[1024,896]{1,0:T(8,128)(2,1)}), bf16[1024,3584]{1,0:T(8,128)(2,1)}) %all-gather.4.cloned.1.call-update) | async-done | bytes 7340048 | tf_op jit(solution)/shard_map/all_gather | solution.py:128
  273.8 13.5 %fusion.1 = f32[8,128,1024]{2,1,0:T(8,128)} fusion(bf16[8,128,3584]{2,1,0:T(8,128)(2,1)} %bitcast.121, bf16[1,3584,1024]{2,1,0:T(8,128)(2,1)} %param.27), kind=kOutput, calls=%fused_computation.6 | convolution fusion | flops 7516192768 | bytes 18874368 | tf_op jit(solution)/shard_map/dot_general | solution.py:127
  287.3 4.7 %all-to-all-start.1 = ((f32[8,128,1024]{2,1,0:T(8,128)}), f32[8,128,1024]{2,1,0:T(8,128)}, u32[]{:S(2)}, u32[]{:S(2)}) async-start(f32[8,128,1024]{2,1,0:T(8,128)} %fusion.1), calls=%async_computation.1 | async-start | bytes 8388608 | tf_op jit(solution)/shard_map/all_to_all | solution.py:132
  292.1 0.6 dynamic-slice
  293.6 8.6 %all-reduce = f32[16]{0:T(128)S(1)} all-reduce(f32[16]{0:T(128)S(1)} %dynamic-update-slice), channel_id=2, replica_groups=mesh['ctx'=4,'exp'=8] {'ctx'}, use_global_device_ids=true, to_apply=%add | all-reduce | flops 16 | bytes 128
  302.5 13.5 %all-gather.1 = f32[16,16,64]{2,1,0:T(8,128)S(1)} all-gather(f32[4,16,64]{2,1,0:T(8,128)S(1)} %get-tuple-element.74), channel_id=3, replica_groups=mesh['ctx'=4,'exp'=8] {'ctx'}, dimensions={0}, use_global_device_ids=true | all-gather | bytes 81920 | tf_op jit(solution)/shard_map/all_gather | solution.py:14
  316.0 0.3 fusion.27
  316.6 0.6 fusion.9
  317.1 0.8 fusion.12
  318.0 0.3 copy.101
  318.3 1.0 reshape.174
  319.3 21.8 %all-to-all-done.1 = f32[8,128,1024]{2,1,0:T(8,128)} async-done(((f32[8,128,1024]{2,1,0:T(8,128)}), f32[8,128,1024]{2,1,0:T(8,128)}, u32[]{:S(2)}, u32[]{:S(2)}) %all-to-all-start.1) | async-done | bytes 4194336 | tf_op jit(solution)/shard_map/all_to_all | solution.py:132
  341.1 2.8 bitcast_reduce_fusion
  343.9 2.0 convolution_convert_fusion.1
  (77 shorter events, 3.6 us)
Async XLA Ops:
  7.2 4.0 %copy-start = (bf16[128,4096]{1,0:T(8,128)(2,1)S(1)}, bf16[128,4096]{1,0:T(8,128)(2,1)}, u32[]{:S(2)}) copy-start(bf16[128,4096]{1,0:T(8,128)(2,1)} %param.22) | copy-start | bytes 3145732
  7.2 266.6 %all-gather.4.cloned.1.call-start = ((), (), s32[]{:S(2)}) async-start(), calls=%async_computation.2 | async-start | bytes 9175040 | tf_op jit(solution)/shard_map/all_gather | solution.py:128
  16.7 114.5 %slice-start = ((s8[7340032]{0:T(1024)(128)(4,1)}), s8[4194304]{0:T(1024)(128)(4,1)S(1)}, s32[]{:S(2)}) async-start(s8[7340032]{0:T(1024)(128)(4,1)} %bitcast.119), calls=%async_computation.3 | async-start | bytes 8388608
  116.2 15.1 %slice-start.1 = ((s8[7340032]{0:T(1024)(128)(4,1)}), s8[3145728]{0:T(1024)(128)(4,1)S(1)}, s32[]{:S(2)}) async-start(s8[7340032]{0:T(1024)(128)(4,1)} %bitcast.119), calls=%async_computation.4 | async-start | bytes 6291456
  131.3 10.5 %copy-start.6 = (f32[4]{0:T(128)S(1)}, f32[4]{0:T(128)}, u32[]{:S(2)}) copy-start(f32[4]{0:T(128)} %param.20) | copy-start | bytes 52
  131.3 10.5 %copy-start.5 = (f32[4,512]{1,0:T(4,128)S(1)}, f32[4,512]{1,0:T(4,128)}, u32[]{:S(2)}) copy-start(f32[4,512]{1,0:T(4,128)} %param.17) | copy-start | bytes 24580
  131.3 14.0 %copy-start.3 = (bf16[16,512]{1,0:T(8,128)(2,1)S(1)}, bf16[16,512]{1,0:T(8,128)(2,1)}, u32[]{:S(2)}) copy-start(bf16[16,512]{1,0:T(8,128)(2,1)} %param.18) | copy-start | bytes 49156
  131.3 14.0 %copy-start.2 = (bf16[512,256]{1,0:T(8,128)(2,1)S(1)}, bf16[512,256]{1,0:T(8,128)(2,1)}, u32[]{:S(2)}) copy-start(bf16[512,256]{1,0:T(8,128)(2,1)} %param.16) | copy-start | bytes 786436
  287.3 4.8 %copy-start.8 = (u32[32]{0:T(128)S(1)}, u32[32]{0:T(128)}, u32[]{:S(2)}) copy-start(u32[32]{0:T(128)} %constant.63) | copy-start | bytes 388
  287.3 14.9 %copy-start.4 = (bf16[16,512]{1,0:T(8,128)(2,1)S(1)}, bf16[16,512]{1,0:T(8,128)(2,1)}, u32[]{:S(2)}) copy-start(bf16[16,512]{1,0:T(8,128)(2,1)} %param.19) | copy-start | bytes 49156
  287.3 29.8 %copy-start.7 = (f32[4]{0:T(128)S(1)}, f32[4]{0:T(128)}, u32[]{:S(2)}) copy-start(f32[4]{0:T(128)} %param.21) | copy-start | bytes 52
  287.3 53.8 %all-to-all-start.1 = ((f32[8,128,1024]{2,1,0:T(8,128)}), f32[8,128,1024]{2,1,0:T(8,128)}, u32[]{:S(2)}, u32[]{:S(2)}) async-start(f32[8,128,1024]{2,1,0:T(8,128)} %fusion.1), calls=%async_computation.1 | async-start | bytes 8388608 | tf_op jit(solution)/shard_map/all_to_all | solution.py:132
  318.3 27.7 %copy-start.1 = (bf16[128,4096]{1,0:T(8,128)(2,1)S(1)}, bf16[128,4096]{1,0:T(8,128)(2,1)}, u32[]{:S(2)}) copy-start(bf16[128,4096]{1,0:T(8,128)(2,1)} %param.22) | copy-start | bytes 3145732
Sparse Core Ops, SparseCore 0:
  141.8 131.9 all-gather.3
where the time goes:
time: 353 us
  waiting for transfers between devices  150 us (42%)
  blocking collectives  122 us (35%)
  matrix products  44.1 us (12%)
  between operations  15 us (4%)
  local copies, waits for them, and re-layouts  9.34 us (3%)
  other arithmetic  8.2 us (2%)
  starting transfers between devices  4.73 us (1%)
    all_gather x1, waiting for transfers between devices, expert_block(): lax.all_gather(hidden, 'ctx', axis=1, tiled=True)  128 us
    all_to_all x1, blocking collectives, expert_block(): lax.all_to_all(doubled.reshape(2 * slot_count, model_width), 'exp', split...  99.4 us
    all_to_all x1, waiting for transfers between devices, expert_block(): lax.all_to_all(partial_out, 'exp', split_axis=0, concat_axis=0, tiled=True)  21.8 us
    dot_general x1, matrix products, expert_block(): up_sums = jnp.dot(arrived, up_weight, preferred_element_type=jnp.float32)  15.1 us
    dot_general x1, matrix products, expert_block(): jnp.dot(lax.all_gather(hidden, 'ctx', axis=1, tiled=True), down_weight, p...  13.5 us
    all_gather x1, blocking collectives, carried_in(): gathered = jax.tree.map(lambda a: lax.all_gather(a, axis), part)  13.5 us
    dot_general x1, matrix products, expert_block(): jnp.dot(arrived, gate_weight, preferred_element_type=jnp.float32)  10.4 us
    unnamed x1, blocking collectives  8.61 us
  transfers between devices with their start and end apart: 2, of which 2 were waited for; matrix products, arithmetic and copies ran while one was open for 2% of the time, Pallas kernels for 0%

commit v1 on v0

--- a/solution.py
+++ b/solution.py
@@ -1,6 +1,10 @@
+import functools
+
 import jax
 import jax.numpy as jnp
 from jax import lax
+from jax.experimental import pallas as pl
+from jax.experimental.pallas import tpu as pltpu
 from jax.sharding import PartitionSpec as P
 
 BLOCK = 256
@@ -137,6 +141,326 @@
     return result.astype(jnp.bfloat16)
 
 
+MESH = pl.DeviceIdType.MESH
+VMEM_BYTES = 60 * 2**20
+GRID = 2
+PAIR = 2
+
+
+def expert_kernel(
+    lines,
+    tok_in,
+    share,
+    gate_hbm,
+    up_hbm,
+    down_hbm,
+    out,
+    gate_w,
+    up_w,
+    down_w,
+    tok,
+    hid,
+    acc,
+    swap,
+    res,
+    ret,
+    load_sem,
+    tsend,
+    trecv,
+    hsend_r,
+    hsend_l,
+    hrecv_l,
+    hrecv_r,
+    xsend,
+    xrecv,
+    rsend,
+    rrecv,
+):
+    chunks = GRID * GRID
+    z = lax.axis_index("ctx")
+    e = lax.axis_index("exp")
+    half = lax.rem(e, PAIR)
+    other = 1 - half
+    px = lax.rem(e // PAIR, GRID)
+    py = e // (PAIR * GRID)
+    rows = tok_in.shape[0]
+    sub = rows // 2
+
+    def peer(c, core):
+        qx = lax.rem(px + lax.rem(c, GRID), GRID)
+        qy = lax.rem(py + c // GRID, GRID)
+        return (z, (qy * GRID + qx) * PAIR + core)
+
+    mine = pl.ds(pl.multiple_of(half * rows, rows), rows)
+    theirs = pl.ds(pl.multiple_of(other * rows, rows), rows)
+    partner = (z, (py * GRID + px) * PAIR + other)
+
+    loads = [
+        pltpu.make_async_copy(gate_hbm, gate_w, load_sem.at[0]),
+        pltpu.make_async_copy(up_hbm, up_w, load_sem.at[1]),
+        pltpu.make_async_copy(tok_in, tok.at[0, mine], load_sem.at[3]),
+        pltpu.make_async_copy(down_hbm, down_w, load_sem.at[2]),
+    ]
+    for load in loads:
+        load.start()
+
+    barrier = pltpu.get_barrier_semaphore()
+    for device in (partner, peer(1, half), peer(2, half), peer(3, half)):
+        pl.semaphore_signal(barrier, inc=1, device_id=device, device_id_type=MESH)
+
+    @pl.when(z > 0)
+    def _():
+        pl.semaphore_signal(barrier, inc=1, device_id=(z - 1, e), device_id_type=MESH)
+
+    @pl.when(z < lines - 1)
+    def _():
+        pl.semaphore_signal(barrier, inc=1, device_id=(z + 1, e), device_id_type=MESH)
+
+    neighbours = 4 + jnp.where(z > 0, 1, 0) + jnp.where(z < lines - 1, 1, 0)
+    pl.semaphore_wait(barrier, neighbours)
+
+    def remote(src, dst, ssem, rsem, device):
+        return pltpu.make_async_remote_copy(
+            src_ref=src,
+            dst_ref=dst,
+            send_sem=ssem,
+            recv_sem=rsem,
+            device_id=device,
+            device_id_type=MESH,
+        )
+
+    upper = pl.ds(pl.multiple_of(half * rows, rows), sub)
+    lower = pl.ds(pl.multiple_of(half * rows + sub, sub), sub)
+    copies = [
+        remote(tok_in, tok.at[0, mine], tsend.at[0], trecv.at[0], partner),
+        remote(tok_in, tok.at[1, mine], tsend.at[1], trecv.at[1], peer(1, half)),
+        remote(tok_in, tok.at[2, mine], tsend.at[2], trecv.at[2], peer(2, half)),
+        remote(
+            tok.at[1, upper], tok.at[3, upper], tsend.at[3], trecv.at[3], peer(2, half)
+        ),
+        remote(
+            tok.at[2, lower], tok.at[3, lower], tsend.at[4], trecv.at[4], peer(1, half)
+        ),
+        remote(tok.at[1, mine], tok.at[1, mine], tsend.at[5], trecv.at[5], partner),
+        remote(tok.at[2, mine], tok.at[2, mine], tsend.at[6], trecv.at[6], partner),
+        remote(tok.at[3, mine], tok.at[3, mine], tsend.at[7], trecv.at[7], partner),
+    ]
+    for copy in copies[:3]:
+        copy.start()
+
+    def make_hidden(c):
+        width = gate_w.shape[1]
+        x = tok[c]
+        g = jnp.dot(x, gate_w[...], preferred_element_type=jnp.float32)
+        u = jnp.dot(x, up_w[...], preferred_element_type=jnp.float32)
+        hid[z, c] = (jax.nn.silu(g) * u).astype(jnp.bfloat16)
+
+    def to_right(d, c):
+        j = z - d
+        return remote(hid.at[j, c], hid.at[j, c], hsend_r.at[d, c], hrecv_l.at[d, c], (z + 1, e))
+
+    def to_left(d, c):
+        j = z + d
+        return remote(hid.at[j, c], hid.at[j, c], hsend_l.at[d, c], hrecv_r.at[d, c], (z - 1, e))
+
+    def from_left(d, c):
+        return remote(
+            hid.at[z - d, c], hid.at[z - d, c], hsend_r.at[d, c], hrecv_l.at[d - 1, c], (z - 1, e)
+        )
+
+    def from_right(d, c):
+        return remote(
+            hid.at[z + d, c], hid.at[z + d, c], hsend_l.at[d, c], hrecv_r.at[d - 1, c], (z + 1, e)
+        )
+
+    def send_own(c):
+        @pl.when(z < lines - 1)
+        def _():
+            to_right(0, c).start()
+
+        @pl.when(z > 0)
+        def _():
+            to_left(0, c).start()
+
+    def pass_on(d, c):
+        @pl.when(z >= d)
+        def _():
+            from_left(d, c).wait_recv()
+
+            @pl.when(z < lines - 1)
+            def _():
+                to_right(d, c).start()
+
+        @pl.when(z + d < lines)
+        def _():
+            from_right(d, c).wait_recv()
+
+            @pl.when(z > 0)
+            def _():
+                to_left(d, c).start()
+
+    def add_down(j, c):
+        acc[c] += jnp.dot(hid[j, c], down_w[j], preferred_element_type=jnp.float32)
+
+    def add_both(d, c):
+        @pl.when(z >= d)
+        def _():
+            add_down(z - d, c)
+
+        @pl.when(z + d < lines)
+        def _():
+            add_down(z + d, c)
+
+    loads[2].wait()
+    loads[0].wait()
+    loads[1].wait()
+    copies[0].wait_recv()
+    make_hidden(0)
+    send_own(0)
+    loads[3].wait()
+
+    def chunk(c, carry):
+        acc[c] = jnp.dot(hid[z, c], down_w[z], preferred_element_type=jnp.float32)
+        pass_on(1, c)
+
+        @pl.when(c == 0)
+        def _():
+            copies[1].wait_recv()
+            copies[5].start()
+            copies[3].start()
+            copies[2].wait_recv()
+            copies[6].start()
+            copies[4].start()
+            copies[5].wait_recv()
+
+        @pl.when(c == 1)
+        def _():
+            copies[3].wait_recv()
+            copies[4].wait_recv()
+            copies[7].start()
+            copies[6].wait_recv()
+
+        @pl.when(c == 2)
+        def _():
+            copies[7].wait_recv()
+
+        @pl.when(c < chunks - 1)
+        def _():
+            make_hidden(c + 1)
+
+        for d in range(2, lines):
+            pass_on(d, c)
+            if d == 2:
+
+                @pl.when(c < chunks - 1)
+                def _():
+                    send_own(c + 1)
+
+            add_both(d - 1, c)
+        add_both(lines - 1, c)
+
+        exchange = remote(acc.at[c, theirs], swap.at[c], xsend.at[c], xrecv.at[c], partner)
+        exchange.start()
+        exchange.wait_recv()
+        res[c] = acc[c, mine] + swap[c]
+
+        @pl.when(c > 0)
+        def _():
+            remote(res.at[c], ret.at[c], rsend.at[c], rrecv.at[c], peer(c, half)).start()
+
+        return carry
+
+    lax.fori_loop(0, chunks, chunk, 0)
+
+    total = share[:, 0:1] * res[0]
+    for c in range(1, chunks):
+        remote(res.at[c], ret.at[c], rsend.at[c], rrecv.at[c], peer(c, half)).wait_recv()
+        total += share[:, c : c + 1] * ret[c]
+    out[...] = total.astype(out.dtype)
+
+    for copy in copies:
+        copy.wait_send()
+    for c in range(chunks):
+        for d in range(lines - 1):
+
+            @pl.when((z >= d) & (z < lines - 1))
+            def _():
+                to_right(d, c).wait_send()
+
+            @pl.when((z + d < lines) & (z > 0))
+            def _():
+                to_left(d, c).wait_send()
+
+        remote(acc.at[c, theirs], swap.at[c], xsend.at[c], xrecv.at[c], partner).wait_send()
+        if c > 0:
+            remote(res.at[c], ret.at[c], rsend.at[c], rrecv.at[c], peer(c, half)).wait_send()
+
+
+def expert_fused(moe_tokens, expert_ids, route_weights, gate_proj, up_proj, down_proj):
+    lines = lax.axis_size("ctx")
+    chunks = GRID * GRID
+    rows, width = moe_tokens.shape
+    part = gate_proj.shape[2]
+    columns = down_proj.shape[2]
+    place = lax.axis_index("exp") // PAIR
+    px, py = place % GRID, place // GRID
+    order = jnp.stack(
+        [((py + c // GRID) % GRID) * GRID + (px + c % GRID) % GRID for c in range(chunks)]
+    )
+    share = jnp.sum(
+        jnp.where(expert_ids[:, :, None] == order[None, None, :], route_weights[:, :, None], 0.0),
+        axis=1,
+    )
+    f32, bf16 = jnp.float32, jnp.bfloat16
+    dma = pltpu.SemaphoreType.DMA
+    vmem = pl.BlockSpec(memory_space=pltpu.VMEM)
+    hbm = pl.BlockSpec(memory_space=pl.ANY)
+    return pl.pallas_call(
+        functools.partial(expert_kernel, lines),
+        out_shape=jax.ShapeDtypeStruct((rows, columns), bf16),
+        in_specs=[vmem, vmem, hbm, hbm, hbm],
+        out_specs=vmem,
+        scratch_shapes=[
+            pltpu.VMEM((width, part), bf16),
+            pltpu.VMEM((width, part), bf16),
+            pltpu.VMEM((lines, part, columns), bf16),
+            pltpu.VMEM((chunks, PAIR * rows, width), bf16),
+            pltpu.VMEM((lines, chunks, PAIR * rows, part), bf16),
+            pltpu.VMEM((chunks, PAIR * rows, columns), f32),
+            pltpu.VMEM((chunks, rows, columns), f32),
+            pltpu.VMEM((chunks, rows, columns), f32),
+            pltpu.VMEM((chunks, rows, columns), f32),
+            dma((4,)),
+            dma((8,)),
+            dma((8,)),
+            dma((lines, chunks)),
+            dma((lines, chunks)),
+            dma((lines, chunks)),
+            dma((lines, chunks)),
+            dma((chunks,)),
+            dma((chunks,)),
+            dma((chunks,)),
+            dma((chunks,)),
+        ],
+        compiler_params=pltpu.CompilerParams(
+            collective_id=0, has_side_effects=True, vmem_limit_bytes=VMEM_BYTES
+        ),
+    )(
+        moe_tokens,
+        share,
+        gate_proj[0],
+        up_proj[0],
+        down_proj[0].reshape(lines, part, columns),
+    )
+
+
+def expert_layer(*arrays):
+    moe_tokens, gate_proj, down_proj = arrays[0], arrays[3], arrays[5]
+    if lax.axis_size("exp") == PAIR * GRID * GRID and gate_proj.shape[2] % 128 == 0:
+        return expert_fused(*arrays)
+    return expert_block(*arrays)
+
+
 def on_device(
     seq_inputs,
     step_size,
@@ -161,7 +485,7 @@
         combine_states,
         (jnp.zeros_like(total_log), jnp.zeros_like(final)),
     )
-    expert_output = expert_block(
+    expert_output = expert_layer(
         moe_tokens, expert_ids, route_weights, gate_proj, up_proj, down_proj
     )
     mixer_output = mixer_finish(

time: 353 us -> 194 us (0.55)
  Pallas kernels: 0 us -> 150 us
  waiting for transfers between devices: 150 us -> 0 us
  blocking collectives: 122 us -> 26.8 us
  matrix products: 44.1 us -> 1.81 us
  between operations: 15 us -> 1.53 us
  starting transfers between devices: 4.73 us -> 0 us
  other arithmetic: 8.2 us -> 4.65 us
    pallas_call x0 -> x1, Pallas kernels: none -> 150 us  [expert_fused(): pl.pallas_call(functools.partial(expert_kernel, lines), out_shape=jax.Sha...]
    all_gather x1 -> x0, waiting for transfers between devices: 128 us -> none  [expert_block(): lax.all_gather(hidden, 'ctx', axis=1, tiled=True)]
    all_to_all x1 -> x0, blocking collectives: 99.4 us -> none  [expert_block(): lax.all_to_all(doubled.reshape(2 * slot_count, model_width), 'exp', split...]
    dot_general x5 -> x0, matrix products: 42.2 us -> none  [the longest x1 15.1 us: expert_block(): up_sums = jnp.dot(arrived, up_weight, preferred_element_type=jnp.float32)]
    all_to_all x1 -> x0, waiting for transfers between devices: 21.8 us -> none  [expert_block(): lax.all_to_all(partial_out, 'exp', split_axis=0, concat_axis=0, tiled=True)]
    unnamed x1, blocking collectives: 8.61 us -> 13.5 us
    all_to_all x1 -> x0, starting transfers between devices: 4.69 us -> none  [expert_block(): lax.all_to_all(partial_out, 'exp', split_axis=0, concat_axis=0, tiled=True)]
    broadcast_in_dim x1 -> x0, local copies, waits for them, and re-layouts: 4.28 us -> none  [expert_block(): jnp.broadcast_to(packed.reshape(expert_count, 1, capacity, model_width),...]
  transfers between devices with their start and end apart: 2 -> 0, of which waited for: 2 -> 0; matrix products, arithmetic and copies ran while one was open for 2% -> 0% of each run, Pallas kernels for 0% -> 0%
where the time goes in v1:
time: 194 us; the launch traced here: 193 us
  Pallas kernels  150 us (77%)
  blocking collectives  26.8 us (14%)
  local copies, waits for them, and re-layouts  8.3 us (4%)
  other arithmetic  4.65 us (2%)
    pallas_call x1, Pallas kernels, expert_fused(): pl.pallas_call(functools.partial(expert_kernel, lines), out_shape=jax.Sha...  150 us
    unnamed x1, blocking collectives  13.5 us
    all_gather x1, blocking collectives, carried_in(): gathered = jax.tree.map(lambda a: lax.all_gather(a, axis), part)  13.4 us
    unnamed x21, local copies, waits for them, and re-layouts  4.05 us

profile of v1, /device:TPU:0, one launch (start us, length us, event | category | flops | bytes accessed | tf_op | source)
XLA Modules:
  0.0 193.1 jit_solution(11155032924968473883)
XLA Ops:
  0.6 0.7 exponential_negate_fusion
  1.3 0.8 broadcast_multiply_fusion
  2.1 2.4 %reduce-window.6 = f32[4,2,2,128]{3,2,1,0:T(2,128)S(1)} reduce-window(f32[4,2,2,128]{3,2,1,0:T(2,128)S(1)} %reshape.104, f32[]{:T(128)} %constant.96.clone.1), window={size=1x1x1x128 pad=0_0x0_0x0_0x127_0}, to_apply=%region_0.0 | reduce-window | flops 260096 | bytes 16388 | tf_op jit(solution)/shard_map/reduce-window
  4.6 0.1 copy.69
  4.8 0.1 copy.70
  5.0 0.2 slice_reduce_fusion
  5.3 1.2 reshape.116
  6.6 0.3 copy.75
  6.9 0.7 mul.109
  7.8 0.7 reshape.103
  8.5 0.2 fusion.11
  8.7 0.2 while.26
  8.9 0.7 dynamic-slice
  10.3 0.2 dynamic-update-slice
  10.5 13.5 %all-reduce = f32[16]{0:T(128)S(1)} all-reduce(f32[16]{0:T(128)S(1)} %dynamic-update-slice), channel_id=2, replica_groups=mesh['ctx'=4,'exp'=8] {'ctx'}, use_global_device_ids=true, to_apply=%add | all-reduce | flops 16 | bytes 128
  24.1 13.4 %all-gather.1 = f32[16,16,64]{2,1,0:T(8,128)S(1)} all-gather(f32[4,16,64]{2,1,0:T(8,128)S(1)} %get-tuple-element.74), channel_id=3, replica_groups=mesh['ctx'=4,'exp'=8] {'ctx'}, dimensions={0}, use_global_device_ids=true | all-gather | bytes 81920 | tf_op jit(solution)/shard_map/all_gather | solution.py:18
  37.5 0.6 fusion.1
  38.1 0.3 fusion.18
  38.4 0.8 fusion.4
  39.2 0.3 copy.90
  39.5 1.0 reshape.115
  40.7 0.7 copy.85.share
  41.5 150.0 %shard_map.131 = bf16[128,1024]{1,0:T(8,128)(2,1)} custom-call(bf16[128,4096]{1,0:T(8,128)(2,1)} %tok_in.1, f32[128,4]{1,0:T(8,128)} %copy.85.share, bf16[4096,896]{1,0:T(8,128)(2,1)} %bitcast.63, bf16[4096,896]{1,0:T(8,128)(2,1)} %bitcast.64, bf16[4,896,1024]{2,1,0:T(8,128)(2,1)} %bitcast.65), custom_call_target="tpu_custom_call" | custom-call | tf_op jit(solution)/shard_map/pallas_call | solution.py:418
  191.5 1.7 copy.128
  (44 shorter events, 1.1 us)
Async XLA Ops:
  0.6 8.3 %copy-start.6 = (u32[32]{0:T(128)S(1)}, u32[32]{0:T(128)}, u32[]{:S(2)}) copy-start(u32[32]{0:T(128)} %constant.111) | copy-start | bytes 388
  2.1 35.4 %copy-start.1 = (bf16[16,512]{1,0:T(8,128)(2,1)S(1)}, bf16[16,512]{1,0:T(8,128)(2,1)}, u32[]{:S(2)}) copy-start(bf16[16,512]{1,0:T(8,128)(2,1)} %param.19) | copy-start | bytes 49156
  6.6 31.5 %copy-start = (bf16[16,512]{1,0:T(8,128)(2,1)S(1)}, bf16[16,512]{1,0:T(8,128)(2,1)}, u32[]{:S(2)}) copy-start(bf16[16,512]{1,0:T(8,128)(2,1)} %param.18) | copy-start | bytes 49156
  6.6 31.8 %copy-start.2 = (f32[4,512]{1,0:T(4,128)S(1)}, f32[4,512]{1,0:T(4,128)}, u32[]{:S(2)}) copy-start(f32[4,512]{1,0:T(4,128)} %param.17) | copy-start | bytes 24580
  6.6 31.8 %copy-start.5 = (f32[4]{0:T(128)S(1)}, f32[4]{0:T(128)}, u32[]{:S(2)}) copy-start(f32[4]{0:T(128)} %param.21) | copy-start | bytes 52
  38.4 2.3 %copy-start.3 = (f32[128,2]{0,1:T(2,128)S(1)}, f32[128,2]{0,1:T(2,128)}, u32[]{:S(2)}) copy-start(f32[128,2]{0,1:T(2,128)} %param.24) | copy-start | bytes 3076
  38.4 2.3 %copy-start.4 = (s32[128,2]{0,1:T(2,128)S(1)}, s32[128,2]{0,1:T(2,128)}, u32[]{:S(2)}) copy-start(s32[128,2]{0,1:T(2,128)} %param.23) | copy-start | bytes 3076

commit v2 on v1

--- a/solution.py
+++ b/solution.py
@@ -11,23 +11,6 @@
 
 
 HIGHEST = lax.Precision.HIGHEST
-
-
-def carried_in(part, axis, combine, identity):
-    place = lax.axis_index(axis)
-    gathered = jax.tree.map(lambda a: lax.all_gather(a, axis), part)
-    state = jax.tree.map(lambda a, e: jnp.zeros_like(a) + jnp.asarray(e, a.dtype), part, identity)
-
-    def one(lap, state):
-        return combine(
-            state, jax.tree.map(lambda a: lax.dynamic_index_in_dim(a, lap, 0, False), gathered)
-        )
-
-    return lax.fori_loop(0, place, one, state)
-
-
-def combine_states(former, latter):
-    return (former[0] + latter[0], jnp.exp(latter[0])[:, None, None] * former[1] + latter[1])
 
 
 def block_chain(running, pieces):
@@ -151,10 +134,12 @@
     lines,
     tok_in,
     share,
+    packed,
     gate_hbm,
     up_hbm,
     down_hbm,
     out,
+    gathered,
     gate_w,
     up_w,
     down_w,
@@ -162,8 +147,13 @@
     hid,
     acc,
     swap,
-    res,
     ret,
+    far_w,
+    acc2,
+    swap2,
+    ret2,
+    edge_in,
+    states,
     load_sem,
     tsend,
     trecv,
@@ -175,6 +165,16 @@
     xrecv,
     rsend,
     rrecv,
+    ssend,
+    srecv,
+    wsend,
+    wrecv,
+    x2send,
+    x2recv,
+    r2send,
+    r2recv,
+    esend,
+    erecv,
 ):
     chunks = GRID * GRID
     z = lax.axis_index("ctx")
@@ -208,16 +208,13 @@
     for device in (partner, peer(1, half), peer(2, half), peer(3, half)):
         pl.semaphore_signal(barrier, inc=1, device_id=device, device_id_type=MESH)
 
-    @pl.when(z > 0)
-    def _():
-        pl.semaphore_signal(barrier, inc=1, device_id=(z - 1, e), device_id_type=MESH)
-
-    @pl.when(z < lines - 1)
-    def _():
-        pl.semaphore_signal(barrier, inc=1, device_id=(z + 1, e), device_id_type=MESH)
-
-    neighbours = 4 + jnp.where(z > 0, 1, 0) + jnp.where(z < lines - 1, 1, 0)
-    pl.semaphore_wait(barrier, neighbours)
+    for j in range(lines):
+
+        @pl.when(z != j)
+        def _():
+            pl.semaphore_signal(barrier, inc=1, device_id=(j, e), device_id_type=MESH)
+
+    pl.semaphore_wait(barrier, 4 + lines - 1)
 
     def remote(src, dst, ssem, rsem, device):
         return pltpu.make_async_remote_copy(
@@ -248,6 +245,39 @@
     for copy in copies[:3]:
         copy.start()
 
+    last = chunks - 1
+    assist = lines > 3
+    edge = (z == 0) | (z == lines - 1)
+    helper = (z == 1) | (z == lines - 2)
+    far = jnp.where(z < 2, lines - 1, 0)
+    piece = far_w.shape[0] // chunks
+
+    def lend(k):
+        span = pl.ds(k * piece, piece)
+        target = jnp.where(z == 0, 1, lines - 2)
+        return remote(
+            down_hbm.at[far, span], far_w.at[span], wsend.at[k], wrecv.at[k], (target, e)
+        )
+
+    def start_lend(k):
+        if assist:
+
+            @pl.when(edge)
+            def _():
+                lend(k).start()
+
+    def state_copy(j):
+        return remote(packed, states.at[z], ssend.at[j], srecv.at[z], (j, e))
+
+    start_lend(0)
+    for j in range(lines):
+
+        @pl.when(z != j)
+        def _():
+            state_copy(j).start()
+
+    states[z] = packed[...]
+
     def make_hidden(c):
         width = gate_w.shape[1]
         x = tok[c]
@@ -282,20 +312,23 @@
         def _():
             to_left(0, c).start()
 
+    def needed(d, c):
+        return (c == last) if assist and d == lines - 1 else True
+
     def pass_on(d, c):
-        @pl.when(z >= d)
+        @pl.when((z >= d) & needed(d, c))
         def _():
             from_left(d, c).wait_recv()
 
-            @pl.when(z < lines - 1)
+            @pl.when((z < lines - 1) & needed(d + 1, c))
             def _():
                 to_right(d, c).start()
 
-        @pl.when(z + d < lines)
+        @pl.when((z + d < lines) & needed(d, c))
         def _():
             from_right(d, c).wait_recv()
 
-            @pl.when(z > 0)
+            @pl.when((z > 0) & needed(d + 1, c))
             def _():
                 to_left(d, c).start()
 
@@ -303,13 +336,23 @@
         acc[c] += jnp.dot(hid[j, c], down_w[j], preferred_element_type=jnp.float32)
 
     def add_both(d, c):
-        @pl.when(z >= d)
+        @pl.when((z >= d) & needed(d, c))
         def _():
             add_down(z - d, c)
 
-        @pl.when(z + d < lines)
+        @pl.when((z + d < lines) & needed(d, c))
         def _():
             add_down(z + d, c)
+
+    def exchange(total, landing, ssem, rsem, c):
+        return remote(total.at[c, theirs], landing.at[c], ssem.at[c], rsem.at[c], partner)
+
+    def bring_home(total, landing, ssem, rsem, c):
+        return remote(total.at[c, mine], landing.at[c], ssem.at[c], rsem.at[c], peer(c, half))
+
+    def end_copy():
+        target = jnp.where(z == 1, 0, lines - 1)
+        return remote(acc2.at[0, mine], edge_in, esend.at[0], erecv.at[0], (target, e))
 
     loads[2].wait()
     loads[0].wait()
@@ -317,6 +360,7 @@
     copies[0].wait_recv()
     make_hidden(0)
     send_own(0)
+    start_lend(1)
     loads[3].wait()
 
     def chunk(c, carry):
@@ -348,6 +392,24 @@
         def _():
             make_hidden(c + 1)
 
+        if assist:
+
+            @pl.when(helper & (c == last))
+            def _():
+                for k in range(chunks):
+                    lend(k).wait_recv()
+                for k in range(last):
+                    acc2[k] = jnp.dot(
+                        hid[far, k], far_w[...], preferred_element_type=jnp.float32
+                    )
+                    exchange(acc2, swap2, x2send, x2recv, k).start()
+                for k in range(1, last):
+                    exchange(acc2, swap2, x2send, x2recv, k).wait_recv()
+                    acc2[k, mine] += swap2[k]
+                    bring_home(acc2, ret2, r2send, r2recv, k).start()
+                exchange(acc2, swap2, x2send, x2recv, 0).wait_recv()
+                acc2[0, mine] = share[:, 0:1] * (acc2[0, mine] + swap2[0])
+
         for d in range(2, lines):
             pass_on(d, c)
             if d == 2:
@@ -356,32 +418,84 @@
                 def _():
                     send_own(c + 1)
 
+                for k in range(2, chunks):
+
+                    @pl.when(c == k - 2)
+                    def _():
+                        start_lend(k)
+
             add_both(d - 1, c)
         add_both(lines - 1, c)
 
-        exchange = remote(acc.at[c, theirs], swap.at[c], xsend.at[c], xrecv.at[c], partner)
-        exchange.start()
-        exchange.wait_recv()
-        res[c] = acc[c, mine] + swap[c]
+        exchange(acc, swap, xsend, xrecv, c).start()
+        exchange(acc, swap, xsend, xrecv, c).wait_recv()
+        acc[c, mine] += swap[c]
 
         @pl.when(c > 0)
         def _():
-            remote(res.at[c], ret.at[c], rsend.at[c], rrecv.at[c], peer(c, half)).start()
+            bring_home(acc, ret, rsend, rrecv, c).start()
+
+        if assist:
+
+            @pl.when(helper & (c == last))
+            def _():
+                for k in range(1, last):
+                    bring_home(acc2, ret2, r2send, r2recv, k).wait_recv()
+                    acc2[0, mine] += share[:, k : k + 1] * ret2[k]
+                end_copy().start()
 
         return carry
 
     lax.fori_loop(0, chunks, chunk, 0)
 
-    total = share[:, 0:1] * res[0]
+    for j in range(lines):
+
+        @pl.when(z != j)
+        def _():
+            remote(packed, states.at[j], ssend.at[j], srecv.at[j], (j, e)).wait_recv()
+
+    gathered[...] = states[...]
+    total = share[:, 0:1] * acc[0, mine]
     for c in range(1, chunks):
-        remote(res.at[c], ret.at[c], rsend.at[c], rrecv.at[c], peer(c, half)).wait_recv()
+        bring_home(acc, ret, rsend, rrecv, c).wait_recv()
         total += share[:, c : c + 1] * ret[c]
-    out[...] = total.astype(out.dtype)
+    swap[0] = total
+    if assist:
+
+        @pl.when(edge)
+        def _():
+            end_copy().wait_recv()
+            swap[0] += edge_in[...]
+
+    out[...] = swap[0].astype(out.dtype)
+
+    for j in range(lines):
+
+        @pl.when(z != j)
+        def _():
+            state_copy(j).wait_send()
+
+    if assist:
+
+        @pl.when(edge)
+        def _():
+            for k in range(chunks):
+                lend(k).wait_send()
+
+        @pl.when(helper)
+        def _():
+            for k in range(last):
+                exchange(acc2, swap2, x2send, x2recv, k).wait_send()
+                if k > 0:
+                    bring_home(acc2, ret2, r2send, r2recv, k).wait_send()
+            end_copy().wait_send()
 
     for copy in copies:
         copy.wait_send()
     for c in range(chunks):
         for d in range(lines - 1):
+            if assist and d == lines - 2 and c < last:
+                continue
 
             @pl.when((z >= d) & (z < lines - 1))
             def _():
@@ -391,12 +505,12 @@
             def _():
                 to_left(d, c).wait_send()
 
-        remote(acc.at[c, theirs], swap.at[c], xsend.at[c], xrecv.at[c], partner).wait_send()
+        exchange(acc, swap, xsend, xrecv, c).wait_send()
         if c > 0:
-            remote(res.at[c], ret.at[c], rsend.at[c], rrecv.at[c], peer(c, half)).wait_send()
-
-
-def expert_fused(moe_tokens, expert_ids, route_weights, gate_proj, up_proj, down_proj):
+            bring_home(acc, ret, rsend, rrecv, c).wait_send()
+
+
+def expert_fused(packed, moe_tokens, expert_ids, route_weights, gate_proj, up_proj, down_proj):
     lines = lax.axis_size("ctx")
     chunks = GRID * GRID
     rows, width = moe_tokens.shape
@@ -417,9 +531,12 @@
     hbm = pl.BlockSpec(memory_space=pl.ANY)
     return pl.pallas_call(
         functools.partial(expert_kernel, lines),
-        out_shape=jax.ShapeDtypeStruct((rows, columns), bf16),
-        in_specs=[vmem, vmem, hbm, hbm, hbm],
-        out_specs=vmem,
+        out_shape=(
+            jax.ShapeDtypeStruct((rows, columns), bf16),
+            jax.ShapeDtypeStruct((lines, *packed.shape), f32),
+        ),
+        in_specs=[vmem, vmem, vmem, hbm, hbm, hbm],
+        out_specs=(vmem, vmem),
         scratch_shapes=[
             pltpu.VMEM((width, part), bf16),
             pltpu.VMEM((width, part), bf16),
@@ -429,7 +546,12 @@
             pltpu.VMEM((chunks, PAIR * rows, columns), f32),
             pltpu.VMEM((chunks, rows, columns), f32),
             pltpu.VMEM((chunks, rows, columns), f32),
-            pltpu.VMEM((chunks, rows, columns), f32),
+            pltpu.VMEM((part, columns), bf16),
+            pltpu.VMEM((chunks - 1, PAIR * rows, columns), f32),
+            pltpu.VMEM((chunks - 1, rows, columns), f32),
+            pltpu.VMEM((chunks - 1, rows, columns), f32),
+            pltpu.VMEM((rows, columns), f32),
+            pltpu.VMEM((lines, *packed.shape), f32),
             dma((4,)),
             dma((8,)),
             dma((8,)),
@@ -441,6 +563,16 @@
             dma((chunks,)),
             dma((chunks,)),
             dma((chunks,)),
+            dma((lines,)),
+            dma((lines,)),
+            dma((chunks,)),
+            dma((chunks,)),
+            dma((chunks,)),
+            dma((chunks,)),
+            dma((chunks,)),
+            dma((chunks,)),
+            dma((1,)),
+            dma((1,)),
         ],
         compiler_params=pltpu.CompilerParams(
             collective_id=0, has_side_effects=True, vmem_limit_bytes=VMEM_BYTES
@@ -448,17 +580,18 @@
     )(
         moe_tokens,
         share,
+        packed,
         gate_proj[0],
         up_proj[0],
         down_proj[0].reshape(lines, part, columns),
     )
 
 
-def expert_layer(*arrays):
+def expert_layer(packed, *arrays):
     moe_tokens, gate_proj, down_proj = arrays[0], arrays[3], arrays[5]
     if lax.axis_size("exp") == PAIR * GRID * GRID and gate_proj.shape[2] % 128 == 0:
-        return expert_fused(*arrays)
-    return expert_block(*arrays)
+        return expert_fused(packed, *arrays)
+    return expert_block(*arrays), lax.all_gather(packed, "ctx")
 
 
 def on_device(
@@ -479,15 +612,19 @@
         seq_inputs, step_size, write_map, read_map, decay_log
     )
     total_log = jnp.sum(block_ends, axis=1)
-    log_before, state_before = carried_in(
-        (total_log, final),
-        "ctx",
-        combine_states,
-        (jnp.zeros_like(total_log), jnp.zeros_like(final)),
-    )
-    expert_output = expert_layer(
-        moe_tokens, expert_ids, route_weights, gate_proj, up_proj, down_proj
-    )
+    head_count, state_count, head_width = final.shape
+    logs = jnp.broadcast_to(total_log[:, None, None], (head_count, 8, head_width))
+    packed = jnp.concatenate([final, logs], axis=1)
+    expert_output, gathered = expert_layer(
+        packed, moe_tokens, expert_ids, route_weights, gate_proj, up_proj, down_proj
+    )
+    place = lax.axis_index("ctx")
+    state_before = jnp.zeros_like(final)
+    for lap in range(lax.axis_size("ctx")):
+        latter = gathered[lap]
+        decay = jnp.exp(latter[:, state_count, 0])
+        added = decay[:, None, None] * state_before + latter[:, :state_count]
+        state_before = jnp.where(lap < place, added, state_before)
     mixer_output = mixer_finish(
         local_mix, cumulative, block_ends, entering, state_before, read_map, seq_inputs, skip_gain
     )

time: 194 us -> 158 us (0.81)
  blocking collectives: 26.8 us -> 0 us
  Pallas kernels: 150 us -> 141 us
    unnamed x1 -> x0, blocking collectives: 13.5 us -> none
    all_gather x1 -> x0, blocking collectives: 13.4 us -> none  [carried_in(): gathered = jax.tree.map(lambda a: lax.all_gather(a, axis), part)]
    pallas_call x1, Pallas kernels: 150 us -> 141 us  [expert_fused(): pl.pallas_call(functools.partial(expert_kernel, lines), out_shape=(jax.Sh...]
    unnamed x21 -> x14, local copies, waits for them, and re-layouts: 4.05 us -> 2.15 us
where the time goes in v2:
time: 158 us
  Pallas kernels  141 us (89%)
  local copies, waits for them, and re-layouts  8.1 us (5%)
  other arithmetic  6.18 us (4%)
  matrix products  1.82 us (1%)
    pallas_call x1, Pallas kernels, expert_fused(): pl.pallas_call(functools.partial(expert_kernel, lines), out_shape=(jax.Sh...  141 us

profile of v2, /device:TPU:0, one launch (start us, length us, event | category | flops | bytes accessed | tf_op | source)
XLA Modules:
  0.0 157.6 jit_solution(8861943934285309079)
XLA Ops:
  0.8 0.7 exponential_negate_fusion
  1.5 0.8 select_reduce_fusion
  2.2 0.8 broadcast_multiply_fusion
  3.0 2.4 %reduce-window.6 = f32[4,2,2,128]{3,2,1,0:T(2,128)S(1)} reduce-window(f32[4,2,2,128]{3,2,1,0:T(2,128)S(1)} %reshape.101, f32[]{:T(128)} %constant.81.clone.1), window={size=1x1x1x128 pad=0_0x0_0x0_0x127_0}, to_apply=%region_0.0 | reduce-window | flops 260096 | bytes 16388 | tf_op jit(solution)/shard_map/reduce-window
  5.9 0.2 slice_reduce_fusion
  6.3 0.7 mul.139
  7.2 0.7 reshape.100
  8.0 0.7 reshape.99
  8.7 0.7 copy.60.share
  9.5 1.2 reshape.106
  10.7 0.3 copy.54
  11.0 0.2 fusion.11
  11.1 0.2 while.13
  11.4 0.6 pad_maximum_fusion.packed
  12.0 140.5 %shard_map.131 = (bf16[128,1024]{1,0:T(8,128)(2,1)}, f32[4,4,24,64]{3,2,1,0:T(8,128)}) custom-call(bf16[128,4096]{1,0:T(8,128)(2,1)} %tok_in.1, f32[128,4]{1,0:T(8,128)} %copy.60.share, f32[4,24,64]{2,1,0:T(8,128)} %pad_maximum_fusion.packed, bf16[4096,896]{1,0:T(8,128)(2,1)} %bitcast.61, bf16[4096,896]{1,0:T(8,128)(2,1)} %bitcast.62, ...), custom_call_target="tpu_custom_call" | custom-call | tf_op jit(solution)/shard_map/pallas_call | solution.py:532
  152.6 0.9 slice_bitcast_fusion
  153.4 0.1 fusion.31
  153.6 0.1 fusion.29
  153.8 0.6 fusion.1
  154.4 0.3 fusion.22
  154.7 0.8 fusion.4
  155.5 0.3 copy.69
  155.8 1.0 reshape.105
  156.9 0.7 copy.100
  (38 shorter events, 1.3 us)
Async XLA Ops:
  12.0 142.4 %copy-start.1 = (bf16[16,512]{1,0:T(8,128)(2,1)S(1)}, bf16[16,512]{1,0:T(8,128)(2,1)}, u32[]{:S(2)}) copy-start(bf16[16,512]{1,0:T(8,128)(2,1)} %param.16) | copy-start | bytes 49156
  12.0 142.4 %copy-start.2 = (bf16[16,512]{1,0:T(8,128)(2,1)S(1)}, bf16[16,512]{1,0:T(8,128)(2,1)}, u32[]{:S(2)}) copy-start(bf16[16,512]{1,0:T(8,128)(2,1)} %param.17) | copy-start | bytes 49156
  12.0 142.6 %copy-start.3 = (f32[4,512]{1,0:T(4,128)S(1)}, f32[4,512]{1,0:T(4,128)}, u32[]{:S(2)}) copy-start(f32[4,512]{1,0:T(4,128)} %param.15) | copy-start | bytes 24580
  12.0 142.7 %copy-start.4 = (f32[4]{0:T(128)S(1)}, f32[4]{0:T(128)}, u32[]{:S(2)}) copy-start(f32[4]{0:T(128)} %param.19) | copy-start | bytes 52
  154.7 2.2 %copy-start = (bf16[128,1024]{1,0:T(8,128)(2,1)S(1)}, bf16[128,1024]{1,0:T(8,128)(2,1)}, u32[]{:S(2)}) copy-start(bf16[128,1024]{1,0:T(8,128)(2,1)} %get-tuple-element.137) | copy-start | bytes 786436

commit v3 on v2

--- a/solution.py
+++ b/solution.py
@@ -26,7 +26,9 @@
     block_count = length // BLOCK
     decay_rate = -jnp.exp(decay_log)
     log_decay = (step_size * decay_rate[:, None]).reshape(head_count, block_count, BLOCK)
-    cumulative = jnp.cumsum(log_decay, axis=2)
+    order = lax.broadcasted_iota(jnp.int32, (BLOCK, BLOCK), 0)
+    until = (order <= lax.broadcasted_iota(jnp.int32, (BLOCK, BLOCK), 1)).astype(jnp.float32)
+    cumulative = jnp.einsum("hks,st->hkt", log_decay, until, precision=HIGHEST)
     block_ends = cumulative[:, :, BLOCK - 1]
     step_blocks = step_size.reshape(head_count, block_count, BLOCK)
     write_blocks = write_map.reshape(state_count, block_count, BLOCK)
@@ -201,7 +203,7 @@
         pltpu.make_async_copy(tok_in, tok.at[0, mine], load_sem.at[3]),
         pltpu.make_async_copy(down_hbm, down_w, load_sem.at[2]),
     ]
-    for load in loads:
+    for load in loads[:3]:
         load.start()
 
     barrier = pltpu.get_barrier_semaphore()
@@ -315,8 +317,8 @@
     def needed(d, c):
         return (c == last) if assist and d == lines - 1 else True
 
-    def pass_on(d, c):
-        @pl.when((z >= d) & needed(d, c))
+    def pass_rightward(d, c, turn):
+        @pl.when((z >= d) & needed(d, c) & turn)
         def _():
             from_left(d, c).wait_recv()
 
@@ -324,13 +326,24 @@
             def _():
                 to_right(d, c).start()
 
-        @pl.when((z + d < lines) & needed(d, c))
+    def pass_leftward(d, c, turn):
+        @pl.when((z + d < lines) & needed(d, c) & turn)
         def _():
             from_right(d, c).wait_recv()
 
             @pl.when((z > 0) & needed(d + 1, c))
             def _():
                 to_left(d, c).start()
+
+    low = z < lines // 2
+
+    def pass_first(d, c):
+        pass_leftward(d, c, low)
+        pass_rightward(d, c, jnp.logical_not(low))
+
+    def pass_second(d, c):
+        pass_rightward(d, c, low)
+        pass_leftward(d, c, jnp.logical_not(low))
 
     def add_down(j, c):
         acc[c] += jnp.dot(hid[j, c], down_w[j], preferred_element_type=jnp.float32)
@@ -357,6 +370,7 @@
     loads[2].wait()
     loads[0].wait()
     loads[1].wait()
+    loads[3].start()
     copies[0].wait_recv()
     make_hidden(0)
     send_own(0)
@@ -365,7 +379,7 @@
 
     def chunk(c, carry):
         acc[c] = jnp.dot(hid[z, c], down_w[z], preferred_element_type=jnp.float32)
-        pass_on(1, c)
+        pass_first(1, c)
 
         @pl.when(c == 0)
         def _():
@@ -391,6 +405,15 @@
         @pl.when(c < chunks - 1)
         def _():
             make_hidden(c + 1)
+            send_own(c + 1)
+
+        for k in range(2, chunks):
+
+            @pl.when(c == k - 2)
+            def _():
+                start_lend(k)
+
+        pass_second(1, c)
 
         if assist:
 
@@ -411,19 +434,8 @@
                 acc2[0, mine] = share[:, 0:1] * (acc2[0, mine] + swap2[0])
 
         for d in range(2, lines):
-            pass_on(d, c)
-            if d == 2:
-
-                @pl.when(c < chunks - 1)
-                def _():
-                    send_own(c + 1)
-
-                for k in range(2, chunks):
-
-                    @pl.when(c == k - 2)
-                    def _():
-                        start_lend(k)
-
+            pass_first(d, c)
+            pass_second(d, c)
             add_both(d - 1, c)
         add_both(lines - 1, c)
 

time: 158 us -> 186 us (1.18)
  Pallas kernels: 141 us -> 172 us
    pallas_call x1, Pallas kernels: 141 us -> 172 us  [expert_fused(): pl.pallas_call(functools.partial(expert_kernel, lines), out_shape=(jax.Sh...]
    another operation x3 -> x0, other arithmetic: 2.54 us -> none
where the time goes in v3:
time: 186 us
  Pallas kernels  172 us (92%)
  local copies, waits for them, and re-layouts  6.84 us (4%)
  other arithmetic  4.38 us (2%)
  matrix products  2 us (1%)
    pallas_call x1, Pallas kernels, expert_fused(): pl.pallas_call(functools.partial(expert_kernel, lines), out_shape=(jax.Sh...  172 us

profile of v3, /device:TPU:0, one launch (start us, length us, event | category | flops | bytes accessed | tf_op | source)
XLA Modules:
  0.0 186.0 jit_solution(6655314390851929349)
XLA Ops:
  0.8 0.7 exponential_negate_fusion
  1.5 0.8 select_reduce_fusion
  2.2 0.8 broadcast_multiply_fusion
  3.0 0.2 fusion.12
  3.2 0.2 slice_reduce_fusion
  3.5 0.8 exponential_multiply_fusion
  4.3 0.7 reshape.54
  5.1 0.7 reshape.53
  5.8 0.7 copy.37.share
  6.6 1.2 reshape.60
  7.8 0.3 copy.34
  8.1 0.2 fusion.14
  8.2 0.2 while.13
  8.5 0.6 pad_maximum_fusion.packed
  9.1 171.9 %shard_map.131 = (bf16[128,1024]{1,0:T(8,128)(2,1)}, f32[4,4,24,64]{3,2,1,0:T(8,128)}) custom-call(bf16[128,4096]{1,0:T(8,128)(2,1)} %tok_in.1, f32[128,4]{1,0:T(8,128)} %copy.37.share, f32[4,24,64]{2,1,0:T(8,128)} %pad_maximum_fusion.packed, bf16[4096,896]{1,0:T(8,128)(2,1)} %bitcast.62, bf16[4096,896]{1,0:T(8,128)(2,1)} %bitcast.63, ...), custom_call_target="tpu_custom_call" | custom-call | tf_op jit(solution)/shard_map/pallas_call | solution.py:544
  181.0 0.9 slice_bitcast_fusion
  181.9 0.1 fusion.34
  182.0 0.1 fusion.32
  182.2 0.6 fusion.1
  182.8 0.3 fusion.25
  183.1 0.8 fusion.4
  183.9 0.3 copy.45
  184.2 1.0 reshape.59
  185.3 0.7 copy.72
  (25 shorter events, 0.5 us)
Async XLA Ops:
  9.1 173.7 %copy-start.1 = (bf16[16,512]{1,0:T(8,128)(2,1)S(1)}, bf16[16,512]{1,0:T(8,128)(2,1)}, u32[]{:S(2)}) copy-start(bf16[16,512]{1,0:T(8,128)(2,1)} %param.16) | copy-start | bytes 49156
  9.1 173.7 %copy-start.2 = (bf16[16,512]{1,0:T(8,128)(2,1)S(1)}, bf16[16,512]{1,0:T(8,128)(2,1)}, u32[]{:S(2)}) copy-start(bf16[16,512]{1,0:T(8,128)(2,1)} %param.17) | copy-start | bytes 49156
  9.1 174.0 %copy-start.3 = (f32[4,512]{1,0:T(4,128)S(1)}, f32[4,512]{1,0:T(4,128)}, u32[]{:S(2)}) copy-start(f32[4,512]{1,0:T(4,128)} %param.15) | copy-start | bytes 24580
  9.1 174.0 %copy-start.4 = (f32[4]{0:T(128)S(1)}, f32[4]{0:T(128)}, u32[]{:S(2)}) copy-start(f32[4]{0:T(128)} %param.19) | copy-start | bytes 52
  183.1 2.2 %copy-start = (bf16[128,1024]{1,0:T(8,128)(2,1)S(1)}, bf16[128,1024]{1,0:T(8,128)(2,1)}, u32[]{:S(2)}) copy-start(bf16[128,1024]{1,0:T(8,128)(2,1)} %get-tuple-element.137) | copy-start | bytes 786436

commit v4 on v2

--- a/solution.py
+++ b/solution.py
@@ -26,7 +26,9 @@
     block_count = length // BLOCK
     decay_rate = -jnp.exp(decay_log)
     log_decay = (step_size * decay_rate[:, None]).reshape(head_count, block_count, BLOCK)
-    cumulative = jnp.cumsum(log_decay, axis=2)
+    order = lax.broadcasted_iota(jnp.int32, (BLOCK, BLOCK), 0)
+    until = (order <= lax.broadcasted_iota(jnp.int32, (BLOCK, BLOCK), 1)).astype(jnp.float32)
+    cumulative = jnp.einsum("hks,st->hkt", log_decay, until, precision=HIGHEST)
     block_ends = cumulative[:, :, BLOCK - 1]
     step_blocks = step_size.reshape(head_count, block_count, BLOCK)
     write_blocks = write_map.reshape(state_count, block_count, BLOCK)
@@ -201,7 +203,7 @@
         pltpu.make_async_copy(tok_in, tok.at[0, mine], load_sem.at[3]),
         pltpu.make_async_copy(down_hbm, down_w, load_sem.at[2]),
     ]
-    for load in loads:
+    for load in loads[:3]:
         load.start()
 
     barrier = pltpu.get_barrier_semaphore()
@@ -357,6 +359,7 @@
     loads[2].wait()
     loads[0].wait()
     loads[1].wait()
+    loads[3].start()
     copies[0].wait_recv()
     make_hidden(0)
     send_own(0)

time: 158 us -> 155 us (0.981)
  other arithmetic: 6.18 us -> 4.38 us
    another operation x3 -> x0, other arithmetic: 2.54 us -> none
where the time goes in v4:
time: 155 us
  Pallas kernels  141 us (91%)
  local copies, waits for them, and re-layouts  6.84 us (4%)
  other arithmetic  4.38 us (3%)
  matrix products  2 us (1%)
    pallas_call x1, Pallas kernels, expert_fused(): pl.pallas_call(functools.partial(expert_kernel, lines), out_shape=(jax.Sh...  141 us

profile of v4, /device:TPU:0, one launch (start us, length us, event | category | flops | bytes accessed | tf_op | source)
XLA Modules:
  0.0 154.7 jit_solution(15490420588411281998)
XLA Ops:
  0.8 0.7 exponential_negate_fusion
  1.5 0.8 select_reduce_fusion
  2.2 0.8 broadcast_multiply_fusion
  3.0 0.2 fusion.12
  3.2 0.2 slice_reduce_fusion
  3.5 0.8 exponential_multiply_fusion
  4.3 0.7 reshape.54
  5.1 0.7 reshape.53
  5.8 0.7 copy.37.share
  6.6 1.2 reshape.60
  7.8 0.3 copy.34
  8.1 0.2 fusion.14
  8.2 0.2 while.13
  8.5 0.6 pad_maximum_fusion.packed
  9.1 140.5 %shard_map.131 = (bf16[128,1024]{1,0:T(8,128)(2,1)}, f32[4,4,24,64]{3,2,1,0:T(8,128)}) custom-call(bf16[128,4096]{1,0:T(8,128)(2,1)} %tok_in.1, f32[128,4]{1,0:T(8,128)} %copy.37.share, f32[4,24,64]{2,1,0:T(8,128)} %pad_maximum_fusion.packed, bf16[4096,896]{1,0:T(8,128)(2,1)} %bitcast.62, bf16[4096,896]{1,0:T(8,128)(2,1)} %bitcast.63, ...), custom_call_target="tpu_custom_call" | custom-call | tf_op jit(solution)/shard_map/pallas_call | solution.py:535
  149.6 0.9 slice_bitcast_fusion
  150.5 0.1 fusion.34
  150.7 0.1 fusion.32
  150.9 0.6 fusion.1
  151.5 0.3 fusion.25
  151.8 0.8 fusion.4
  152.6 0.3 copy.45
  152.9 1.0 reshape.59
  153.9 0.7 copy.72
  (25 shorter events, 0.5 us)
Async XLA Ops:
  9.1 142.4 %copy-start.1 = (bf16[16,512]{1,0:T(8,128)(2,1)S(1)}, bf16[16,512]{1,0:T(8,128)(2,1)}, u32[]{:S(2)}) copy-start(bf16[16,512]{1,0:T(8,128)(2,1)} %param.16) | copy-start | bytes 49156
  9.1 142.4 %copy-start.2 = (bf16[16,512]{1,0:T(8,128)(2,1)S(1)}, bf16[16,512]{1,0:T(8,128)(2,1)}, u32[]{:S(2)}) copy-start(bf16[16,512]{1,0:T(8,128)(2,1)} %param.17) | copy-start | bytes 49156
  9.1 142.6 %copy-start.3 = (f32[4,512]{1,0:T(4,128)S(1)}, f32[4,512]{1,0:T(4,128)}, u32[]{:S(2)}) copy-start(f32[4,512]{1,0:T(4,128)} %param.15) | copy-start | bytes 24580
  9.1 142.7 %copy-start.4 = (f32[4]{0:T(128)S(1)}, f32[4]{0:T(128)}, u32[]{:S(2)}) copy-start(f32[4]{0:T(128)} %param.19) | copy-start | bytes 52
  151.8 2.2 %copy-start = (bf16[128,1024]{1,0:T(8,128)(2,1)S(1)}, bf16[128,1024]{1,0:T(8,128)(2,1)}, u32[]{:S(2)}) copy-start(bf16[128,1024]{1,0:T(8,128)(2,1)} %get-tuple-element.137) | copy-start | bytes 786436
